TPU v7x, 32 devices: a whole 2x2x4 slice. The times are simulated.
32 devices in a mesh: dp: 8 (over y, x, core), own: 4 (over z).
Axes of the slice: x: 2, y: 2, z: 4, core: 2. Of those that a mesh axis runs over, the one named last changes fastest.
Arguments:
- grad: bfloat16 [8192, 1024], P(('dp', 'own')), may hold values from -88 to 88
- left_stats: float32 [8, 1024, 1024], P('dp', 'own'), may hold values from -0.4 to 2.6
- right_stats: float32 [8, 1024, 1024], P('dp', 'own'), may hold values from -0.4 to 2.6
- left_roots: float32 [8, 1024, 1024], P('dp', 'own'), may hold values from -0.4 to 2.6, as said below
- right_roots: float32 [8, 1024, 1024], P('dp', 'own'), may hold values from -0.4 to 2.6, as said below
Outputs:
- direction: bfloat16 [8192, 1024], P(('dp', 'own'))
- left_new: float32 [8, 1024, 1024], P('dp', 'own')
- right_new: float32 [8, 1024, 1024], P('dp', 'own')
Inputs may be any that keep to these rules, and one draw needn't show every extreme that they name: `right_roots`: each block's feature-side root is symmetric. `left_roots`: each block's vocabulary-side root is symmetric.
All inputs are finite; a program needn't handle non-finite values.
Results may differ from a plain program's by a relative error of at most 0.0049.
Values may be sent and summed in bfloat16 or wider, within the bound.
No kernel may reach another device: no remote copies, remote signals or barrier semaphores. Data moves between devices by JAX's collectives and lax.ppermute only.
A program may use at most 64 MiB of HBM per device.

v0:
```python
import jax
import jax.numpy as jnp
from jax import lax
from jax.sharding import PartitionSpec as P

highest = lax.Precision.HIGHEST
epsilon = 1e-06


def transpose_product(left_side, right_side):
    return lax.dot_general(
        left_side, right_side, (((0,), (0,)), ((), ())), preferred_element_type=jnp.float32
    )


def local(grad, left_stats, right_stats, left_roots, right_roots):
    feature_width = grad.shape[1]
    owner_count = lax.axis_size("own")
    slice_width = feature_width // owner_count
    own_rows = grad.astype(jnp.float32)
    grad_square = jnp.sum(own_rows * own_rows)
    whole_grad = lax.all_gather(grad, "own", axis=0, tiled=True)
    feature_cols = lax.dynamic_slice_in_dim(
        whole_grad, lax.axis_index("own") * slice_width, slice_width, 1
    )
    left_gram = lax.dot_general(
        grad, whole_grad, (((1,), (1,)), ((), ())), preferred_element_type=jnp.float32
    )
    right_gram = transpose_product(feature_cols, whole_grad)
    left_update = 0.9 * left_stats[0] + 0.1 / feature_width * left_gram
    right_update = 0.9 * right_stats[0] + 0.1 / feature_width * right_gram
    mixed_cols = lax.dot_general(
        whole_grad.astype(jnp.float32), right_roots[0], (((1,), (1,)), ((), ())), precision=highest
    )
    mixed_cols = mixed_cols.astype(jnp.bfloat16)
    precond = jnp.dot(
        left_roots[0],
        lax.all_gather(mixed_cols, "own", axis=1, tiled=True).astype(jnp.float32),
        precision=highest,
    )
    precond_square = jnp.sum(precond * precond)
    norm_totals = lax.psum((grad_square, precond_square), "own")
    graft_scale = jnp.sqrt(norm_totals[0] / (norm_totals[1] + epsilon))
    direction = (precond * graft_scale).astype(jnp.bfloat16)
    return (direction, left_update[None], right_update[None])


def solution(mesh):
    in_specs = (
        P(("dp", "own"), None),
        P("dp", "own", None),
        P("dp", "own", None),
        P("dp", "own", None),
        P("dp", "own", None),
    )
    out_specs = (P(("dp", "own"), None), P("dp", "own", None), P("dp", "own", None))
    return jax.shard_map(local, mesh=mesh, in_specs=in_specs, out_specs=out_specs, check_vma=False)
```

profile of v0, /device:TPU:0, one launch (start us, length us, event | category | flops | bytes accessed | tf_op | source)
XLA Modules:
  0.0 131.7 jit_solution(18139367668326251888)
XLA Ops:
  7.2 0.0 copy-start
  7.2 0.0 all-gather.3.cloned.1.call-start
  7.2 0.7 all-gather.3.cloned.1.call-update
  7.9 0.0 all-gather.5.cloned.1.call-start
  8.0 50.0 %all-gather.3.cloned.1.call-done = bf16[1024,1024]{1,0:T(8,128)(2,1)} async-done(((bf16[256,1024]{1,0:T(8,128)(2,1)}), bf16[1024,1024]{1,0:T(8,128)(2,1)}) %all-gather.3.cloned.1.call-update) | async-done | bytes 2097168 | tf_op jit(solution)/shard_map/all_gather | solution.py:22
  58.0 0.0 copy-start.1
  58.0 4.7 %convolution_convert_fusion = bf16[1024,256]{1,0:T(8,128)(2,1)} fusion(bf16[1024,1024]{1,0:T(8,128)(2,1)} %all-gather.3.cloned.1.call-done, f32[1,256,1024]{2,1,0:T(8,128)} %param.9), kind=kOutput, calls=%fused_computation.6 | convolution fusion | flops 3221487616 | bytes 3670016 | tf_op jit(solution)/shard_map/dot_general | solution.py:32
  62.6 0.0 all-gather.5.cloned.1.call-update
  62.7 1.9 %multiply_reduce_fusion.1 = f32[]{:T(128)} fusion(bf16[256,1024]{1,0:T(8,128)(2,1)} %param.5), kind=kLoop, calls=%fused_computation.12 | loop fusion | flops 786431 | bytes 524292 | tf_op jit(solution)/shard_map/reduce_sum | solution.py:21
  64.6 0.0 copy-done.1
  64.6 0.0 copy-start.2
  64.6 0.0 copy-start.3
  64.6 3.1 %fusion.1 = f32[1,256,1024]{2,1,0:T(8,128)} fusion(bf16[1024,1024]{1,0:T(8,128)(2,1)S(1)} %copy-done.1, f32[1,256,1024]{2,1,0:T(8,128)} %param.7, s32[]{:T(128)S(6)} %select_n.3), kind=kOutput, calls=%fused_computation.2 | convolution fusion | flops 537657344 | bytes 4718596 | tf_op jit(solution)/shard_map/dot_general | solution.py:11
  67.7 0.0 copy-done.2
  67.7 0.0 copy-done.3
  67.7 1.8 %fusion.3 = f32[1,256,1024]{2,1,0:T(8,128)} fusion(bf16[256,1024]{1,0:T(8,128)(2,1)S(1)} %copy-done.2, bf16[1024,1024]{1,0:T(8,128)(2,1)S(1)} %copy-done.1, f32[1,256,1024]{2,1,0:T(8,128)S(1)} %copy-done.3), kind=kOutput, calls=%fused_computation.5 | convolution fusion | flops 537657344 | bytes 4718592 | tf_op jit(solution)/shard_map/dot_general | solution.py:26
  69.4 38.4 %all-gather.5.cloned.1.call-done = bf16[1024,1024]{1,0:T(8,128)(2,1)} async-done(((bf16[1024,256]{1,0:T(8,128)(2,1)}), bf16[1024,1024]{1,0:T(8,128)(2,1)}) %all-gather.5.cloned.1.call-update) | async-done | bytes 2097168 | tf_op jit(solution)/shard_map/all_gather | solution.py:38
  107.9 0.0 copy-done
  107.9 4.6 %multiply_reduce_fusion = (f32[]{:T(128)}, f32[1024,256]{1,0:T(8,128)S(1)}) fusion(bf16[1024,1024]{1,0:T(8,128)(2,1)} %all-gather.5.cloned.1.call-done, f32[1,256,1024]{2,1,0:T(8,128)S(1)} %copy-done), kind=kOutput, calls=%fused_computation.11 | convolution fusion | flops 3221749760 | bytes 4194308 | tf_op jit(solution)/shard_map/dot_general | solution.py:36
  112.4 10.0 %all-reduce = (f32[]{:T(128)}, f32[]{:T(128)}) all-reduce(f32[]{:T(128)} %multiply_reduce_fusion.1, f32[]{:T(128)} %get-tuple-element.8), channel_id=1, replica_groups=mesh['dp'=8,'own'=4] {'own'}, use_global_device_ids=true, to_apply=%region_1.0 | all-reduce | flops 2 | bytes 16 | tf_op jit(solution)/shard_map/psum | solution.py:42
  123.7 0.1 fusion.7
  123.9 1.0 copy.8
Async XLA Ops:
  7.2 100.7 %copy-start = (f32[1,256,1024]{2,1,0:T(8,128)S(1)}, f32[1,256,1024]{2,1,0:T(8,128)}, u32[]{:S(2)}) copy-start(f32[1,256,1024]{2,1,0:T(8,128)} %param.8) | copy-start | bytes 3145732
  7.2 50.8 %all-gather.3.cloned.1.call-start = ((), (), s32[]{:S(2)}) async-start(), calls=%async_computation | async-start | bytes 2621440 | tf_op jit(solution)/shard_map/all_gather | solution.py:22
  7.9 100.0 %all-gather.5.cloned.1.call-start = ((), (), s32[]{:S(2)}) async-start(), calls=%async_computation.1 | async-start | bytes 2621440 | tf_op jit(solution)/shard_map/all_gather | solution.py:38
  58.0 6.6 %copy-start.1 = (bf16[1024,1024]{1,0:T(8,128)(2,1)S(1)}, bf16[1024,1024]{1,0:T(8,128)(2,1)}, u32[]{:S(2)}) copy-start(bf16[1024,1024]{1,0:T(8,128)(2,1)} %all-gather.3.cloned.1.call-done) | copy-start | bytes 6291460
  64.6 3.1 %copy-start.2 = (bf16[256,1024]{1,0:T(8,128)(2,1)S(1)}, bf16[256,1024]{1,0:T(8,128)(2,1)}, u32[]{:S(2)}) copy-start(bf16[256,1024]{1,0:T(8,128)(2,1)} %param.5) | copy-start | bytes 1572868
  64.6 3.1 %copy-start.3 = (f32[1,256,1024]{2,1,0:T(8,128)S(1)}, f32[1,256,1024]{2,1,0:T(8,128)}, u32[]{:S(2)}) copy-start(f32[1,256,1024]{2,1,0:T(8,128)} %param.6) | copy-start | bytes 3145732
Sparse Core Ops, SparseCore 0:
  9.6 48.3 all-gather.2
  62.8 45.0 all-gather.4
where the time goes:
time: 132 us
  waiting for transfers between devices  89.2 us (68%)
  between operations  15.3 us (12%)
  matrix products  14.1 us (11%)
  blocking collectives  10 us (8%)
  other arithmetic  2.01 us (2%)
    all_gather x1, waiting for transfers between devices, local(): whole_grad = lax.all_gather(grad, 'own', axis=0, tiled=True)  50 us
    all_gather x1, waiting for transfers between devices, local(): lax.all_gather(mixed_cols, 'own', axis=1, tiled=True).astype(jnp.float32)  38.4 us
    psum x1, blocking collectives, local(): norm_totals = lax.psum((grad_square, precond_square), 'own')  10 us
    dot_general x1, matrix products, local(): lax.dot_general(whole_grad.astype(jnp.float32), right_roots[0], (((1,), (...  4.66 us
    dot_general x1, matrix products, local(): jnp.dot(left_roots[0], lax.all_gather(mixed_cols, 'own', axis=1, tiled=Tr...  4.57 us
    dot_general x1, matrix products, transpose_product(): lax.dot_general(left_side, right_side, (((0,), (0,)), ((), ())), preferre...  3.07 us
  transfers between devices with their start and end apart: 2, of which 2 were waited for; matrix products, arithmetic and copies ran while one was open for 5% of the time, Pallas kernels for 0%

commit v1 on v0

v1 whole, which is shorter than its diff:
```python
import jax
import jax.numpy as jnp
from jax import lax
from jax.experimental import pallas as pl
from jax.experimental.pallas import tpu as pltpu
from jax.sharding import PartitionSpec as P


highest = lax.Precision.HIGHEST
epsilon = 1e-06

pair_swap = ((0, 1), (1, 0), (2, 3), (3, 2))
middle_swap = ((1, 2), (2, 1))
outward_in = ((0, 1), (3, 2))
inward_out = ((1, 0), (2, 3))
across_out = ((2, 0), (1, 3))


def send(value, pairs):
    return lax.ppermute(value, "own", pairs)


def contract(left_side, right_side, left_dim, right_dim):
    return lax.dot_general(
        left_side,
        right_side,
        (((left_dim,), (right_dim,)), ((), ())),
        preferred_element_type=jnp.float32,
    )


def split(value):
    high = value.astype(jnp.bfloat16)
    return high, (value - high.astype(jnp.float32)).astype(jnp.bfloat16)


def square_sum(value):
    wide = value.astype(jnp.float32)
    return jnp.sum(wide * wide)


def statistics(grad, whole_grad, left_stats, right_stats):
    feature_width = whole_grad.shape[1]
    slice_width = feature_width // lax.axis_size("own")
    feature_cols = lax.dynamic_slice_in_dim(
        whole_grad, lax.axis_index("own") * slice_width, slice_width, 1
    )
    left_gram = contract(grad, whole_grad, 1, 1)
    right_gram = contract(feature_cols, whole_grad, 0, 0)
    left_update = 0.9 * left_stats[0] + 0.1 / feature_width * left_gram
    right_update = 0.9 * right_stats[0] + 0.1 / feature_width * right_gram
    return left_update[None], right_update[None]


def gathered(grad, left_stats, right_stats, left_roots, right_roots):
    whole_grad = lax.all_gather(grad, "own", axis=0, tiled=True)
    left_update, right_update = statistics(grad, whole_grad, left_stats, right_stats)
    mixed_cols = lax.dot_general(
        whole_grad.astype(jnp.float32), right_roots[0], (((1,), (1,)), ((), ())), precision=highest
    ).astype(jnp.bfloat16)
    precond = jnp.dot(
        left_roots[0],
        lax.all_gather(mixed_cols, "own", axis=1, tiled=True).astype(jnp.float32),
        precision=highest,
    )
    norm_totals = lax.psum((square_sum(grad), square_sum(precond)), "own")
    graft_scale = jnp.sqrt(norm_totals[0] / (norm_totals[1] + epsilon))
    return (precond * graft_scale).astype(jnp.bfloat16), left_update, right_update


def places():
    me = lax.axis_index("own")
    is_end = (me == 0) | (me == 3)
    partner = me + 1 - 2 * lax.rem(me, 2)
    end = jnp.where(is_end, me, partner)
    middle = jnp.where(is_end, partner, me)
    return is_end, end, middle, 3 - middle, 3 - end


def band(place, width):
    return pl.ds(pl.multiple_of(place * width, width), width)


def call(kernel, outs, *operands, flops=10**9, scratch=()):
    moved = sum(o.size * o.dtype.itemsize for o in (*operands, *outs))
    return pl.pallas_call(
        kernel,
        out_shape=outs,
        in_specs=[pl.BlockSpec(memory_space=pltpu.VMEM)] * len(operands),
        out_specs=[pl.BlockSpec(memory_space=pltpu.VMEM)] * len(outs),
        scratch_shapes=scratch,
        compiler_params=pltpu.CompilerParams(vmem_limit_bytes=24 * 2**20),
        cost_estimate=pl.CostEstimate(flops=flops, bytes_accessed=moved, transcendentals=0),
    )(*operands)


def shape(dims, dtype):
    return jax.ShapeDtypeStruct(dims, dtype)


def mix_rows(blocks, high, low, out):
    width = high.shape[0]
    for i, block in enumerate(blocks):
        value = block[...]
        mixed = contract(value, high[...], 1, 1) + contract(value, low[...], 1, 1)
        out[i * width : (i + 1) * width, :] = mixed.astype(out.dtype)


def mix_own_kernel(*refs):
    *blocks, roots, out, high, low = refs
    high[...], low[...] = split(roots[...])
    mix_rows(blocks, high, low, out)


def fill_end(width, end, middle, near, received, high, low, first):
    rows = pl.ds(first, width)
    high[rows, :width], low[rows, :width] = split(received[:, :width])
    high[rows, 3 * width :], low[rows, 3 * width :] = split(received[:, 2 * width :])
    cols = band(jnp.where(middle == 1, 2, 1), width)
    high[rows, cols], low[rows, cols] = split(received[:, width : 2 * width])
    cols = band(jnp.where(middle == 1, 1, 2), width)
    high[rows, cols], low[rows, cols] = split(near[:, band(end, width)].T)


def mix_end_kernel(end_block, middle_block, other_block, last_block, roots, received, out, high, low):
    _, end, middle, _, _ = places()
    fill_end(roots.shape[0], end, middle, roots, received, high, low, 0)
    mix_rows((end_block, middle_block, other_block, last_block), high, low, out)


def fill_both(roots, received, high, low):
    width = roots.shape[0]
    _, end, middle, _, _ = places()
    high[:width, :], low[:width, :] = split(roots[...])
    fill_end(width, end, middle, roots, received, high, low, width)


def gather_rows(pieces, order, rows):
    width = rows.shape[1]
    start = 0
    for place in order:
        piece, offset = pieces[0], start
        rows[band(place, width), :] = piece[offset : offset + width, :]
        start += width
        if start == piece.shape[0]:
            pieces, start = pieces[1:], 0


def first_kernel(
    roots, received, of_end, middle_near, middle_far, other_near, other_far, kept, back, square, high, low, *rows
):
    width = roots.shape[0]
    _, end, middle, other, last = places()
    fill_both(roots, received, high, low)
    total = jnp.zeros((1, width), jnp.float32)
    near, far = (end, middle, other, last), (last, other, middle, end)
    columns = (
        ((of_end,), near),
        ((middle_near, middle_far), near),
        ((other_near, other_far), far),
    )
    for i, (pieces, order) in enumerate(columns):
        gather_rows(pieces, order, rows[i])
        value = rows[i][...]
        pre = contract(high[...], value, 1, 0) + contract(low[...], value, 1, 0)
        kept[:, i * width : (i + 1) * width] = pre[:width]
        back[:, i * width : (i + 1) * width] = pre[width:].astype(back.dtype)
        total += jnp.sum(pre * pre, axis=0, keepdims=True)
    square[...] = jnp.broadcast_to(jnp.sum(total, keepdims=True), square.shape)


def second_kernel(roots, received, of_last, before, kept, back, square, high, low, rows):
    width = roots.shape[0]
    _, end, middle, other, last = places()
    fill_both(roots, received, high, low)
    gather_rows((of_last,), (last, other, middle, end), rows)
    value = rows[...]
    pre = contract(high[...], value, 1, 0) + contract(low[...], value, 1, 0)
    back[:width, :] = pre[width:].astype(back.dtype)
    kept[...] = pre[:width]
    total = jnp.sum(jnp.sum(pre * pre, axis=0, keepdims=True), keepdims=True)
    total = before[...] + jnp.broadcast_to(total, square.shape)
    square[...] = total
    terms = jnp.broadcast_to(total[0:1, 0:1], (back.shape[0] - width, width))
    row = lax.broadcasted_iota(jnp.int32, terms.shape, 0)
    top = terms.astype(jnp.bfloat16).astype(jnp.float32)
    mid = (terms - top).astype(jnp.bfloat16).astype(jnp.float32)
    terms = jnp.where(row == 0, top, jnp.where(row == 1, mid, terms - top - mid))
    back[width:, :] = terms.astype(back.dtype)


def statistics_kernel(
    own, partner, across, far, in_across, in_far, left_stats, right_stats, left, right, square, whole
):
    width, feature_width = own.shape
    is_end, end, middle, other, last = places()
    me = lax.axis_index("own")
    whole[band(me, width), :] = own[...]
    whole[band(jnp.where(is_end, middle, end), width), :] = partner[...]
    whole[band(other, width), :] = jnp.where(is_end, in_across[...], across[...])
    whole[band(last, width), :] = jnp.where(is_end, in_far[...], far[...])
    rate = 0.1 / feature_width
    total = jnp.zeros((1, feature_width), jnp.float32)
    for i in range(feature_width // width):
        cols = slice(i * width, (i + 1) * width)
        rows = whole[cols, :]
        left[:, cols] = 0.9 * left_stats[:, cols] + rate * contract(own[...], rows, 1, 1)
        wide = rows.astype(jnp.float32)
        total += jnp.sum(wide * wide, axis=0, keepdims=True)
    mine = whole[:, band(me, width)]
    right[...] = 0.9 * right_stats[...] + rate * contract(mine, whole[...], 0, 0)
    square[...] = jnp.broadcast_to(jnp.sum(total, keepdims=True), square.shape)


def scale_kernel(
    kept, kept_last, back, back_last, square, square_across, square_far, grad_square, out
):
    width = out.shape[0]
    is_end, *order = places()
    pieces = [slice(i * width, (i + 1) * width) for i in range(3)]

    def factor(near, far):
        return jnp.sqrt(grad_square[0:1, 0:1] / (near + far + epsilon))

    @pl.when(is_end)
    def _():
        terms = back_last[width:, 0:1].astype(jnp.float32)
        scale = factor(terms[0:1] + terms[1:2] + terms[2:3], square_far[0:1, 0:1])
        for place, cols in zip(order, pieces):
            value = back[:, cols].astype(jnp.float32) * scale
            out[:, band(place, width)] = value.astype(out.dtype)
        value = back_last[:width, :].astype(jnp.float32) * scale
        out[:, band(order[3], width)] = value.astype(out.dtype)

    @pl.when(jnp.logical_not(is_end))
    def _():
        scale = factor(square[0:1, 0:1], square_across[0:1, 0:1])
        for place, cols in zip(order, pieces):
            out[:, band(place, width)] = (kept[:, cols] * scale).astype(out.dtype)
        out[:, band(order[3], width)] = (kept_last[...] * scale).astype(out.dtype)


def ordered(grad, left_stats, right_stats, left_roots, right_roots):
    width, feature_width = grad.shape
    is_low = lax.axis_index("own") < 2
    bf16, f32 = jnp.bfloat16, jnp.float32
    left_roots, right_roots = left_roots[0], right_roots[0]

    def three_blocks(roots):
        inner = lax.dynamic_slice_in_dim(roots, jnp.where(is_low, 2, 1) * width, width, 1)
        return jnp.concatenate([roots[:, :width], inner, roots[:, 3 * width :]], 1)

    partner = send(grad, pair_swap)
    across = send(grad, middle_swap)
    end_right = send(three_blocks(right_roots), outward_in)
    end_left = send(three_blocks(left_roots), outward_in)
    far = send(partner, middle_swap)
    halves = [pltpu.VMEM((width, feature_width), bf16)] * 2
    stacked = [pltpu.VMEM((2 * width, feature_width), bf16)] * 2
    column = [pltpu.VMEM((feature_width, width), bf16)]
    rest = feature_width - width
    near_out, far_out = [shape((rest, width), bf16)], [shape((width, width), bf16)]
    (near_mixed,) = call(
        mix_own_kernel, near_out, partner, grad, across, right_roots, scratch=halves
    )
    in_across = send(across, inward_out)
    other_near = send(near_mixed, middle_swap)
    (far_mixed,) = call(mix_own_kernel, far_out, far, right_roots, scratch=halves)
    other_far = send(far_mixed, middle_swap)
    in_far = send(far, inward_out)
    (of_end,) = call(
        mix_end_kernel,
        [shape((feature_width, width), bf16)],
        partner,
        grad,
        across,
        far,
        right_roots,
        end_right,
        scratch=halves,
    )
    of_last = send(of_end, middle_swap)
    left_new, right_new, grad_square = call(
        statistics_kernel,
        [shape((width, feature_width), f32)] * 2 + [shape((8, 128), f32)],
        grad,
        partner,
        across,
        far,
        in_across,
        in_far,
        left_stats[0],
        right_stats[0],
        scratch=[pltpu.VMEM((feature_width, feature_width), bf16)],
    )
    kept, back, square = call(
        first_kernel,
        [shape((width, rest), f32), shape((width, rest), bf16), shape((8, 128), f32)],
        left_roots,
        end_left,
        of_end,
        near_mixed,
        far_mixed,
        other_near,
        other_far,
        scratch=stacked + 3 * column,
    )
    back = send(back, inward_out)
    kept_last, back_last, square = call(
        second_kernel,
        [shape((width, width), f32), shape((width + 16, width), bf16), shape((8, 128), f32)],
        left_roots,
        end_left,
        of_last,
        square,
        scratch=stacked + column,
    )
    back_last = send(back_last, inward_out)
    square_across = send(square, middle_swap)
    square_far = send(square, across_out)
    (direction,) = call(
        scale_kernel,
        [shape((width, feature_width), bf16)],
        kept,
        kept_last,
        back,
        back_last,
        square,
        square_across,
        square_far,
        grad_square,
        flops=10**6,
    )
    return direction, left_new[None], right_new[None]


def solution(mesh):
    in_specs = (
        P(("dp", "own"), None),
        P("dp", "own", None),
        P("dp", "own", None),
        P("dp", "own", None),
        P("dp", "own", None),
    )
    out_specs = (P(("dp", "own"), None), P("dp", "own", None), P("dp", "own", None))
    specs = {"mesh": mesh, "in_specs": in_specs, "out_specs": out_specs, "check_vma": False}
    if mesh.shape["own"] != 4:
        return jax.shard_map(gathered, **specs)
    return jax.shard_map(ordered, **specs)
```

time: 132 us -> 75.5 us (0.57)
  waiting for transfers between devices: 89.2 us -> 41.1 us
  starting transfers between devices: 0.08 us -> 21.6 us
  between operations: 15.3 us -> 0.92 us
  matrix products: 14.1 us -> 0 us
  blocking collectives: 10 us -> 0 us
  Pallas kernels: 0 us -> 9.31 us
  other arithmetic: 2.01 us -> 0.11 us
    all_gather x2 -> x0, waiting for transfers between devices: 88.5 us -> none  [the longest x1 50 us: local(): whole_grad = lax.all_gather(grad, 'own', axis=0, tiled=True)]
    ppermute x0 -> x14, waiting for transfers between devices: none -> 41.1 us  [send(): return lax.ppermute(value, 'own', pairs)]
    ppermute x0 -> x14, starting transfers between devices: none -> 21.6 us  [send(): return lax.ppermute(value, 'own', pairs)]
    dot_general x4 -> x0, matrix products: 14.1 us -> none  [the longest x1 4.66 us: local(): lax.dot_general(whole_grad.astype(jnp.float32), right_roots[0], (((1,), (...]
    psum x1 -> x0, blocking collectives: 10 us -> none  [local(): norm_totals = lax.psum((grad_square, precond_square), 'own')]
    pallas_call x0 -> x7, Pallas kernels: none -> 9.31 us  [call(): pl.pallas_call(kernel, out_shape=outs, in_specs=[pl.BlockSpec(memory_spac...]
    reduce_sum x1 -> x0, other arithmetic: 1.91 us -> none  [local(): grad_square = jnp.sum(own_rows * own_rows)]
  transfers between devices with their start and end apart: 2 -> 14, of which waited for: 2 -> 6; matrix products, arithmetic and copies ran while one was open for 5% -> 3% of each run, Pallas kernels for 0% -> 11%
where the time goes in v1:
time: 75.5 us; the launch traced here: 75.1 us
  waiting for transfers between devices  41.1 us (54%)
  starting transfers between devices  21.6 us (29%)
  Pallas kernels  9.31 us (12%)
  local copies, waits for them, and re-layouts  2.14 us (3%)
  between operations  0.92 us (1%)
    ppermute x14, waiting for transfers between devices, send(): return lax.ppermute(value, 'own', pairs)  41.1 us
    ppermute x14, starting transfers between devices, send(): return lax.ppermute(value, 'own', pairs)  21.6 us
    pallas_call x7, Pallas kernels, call(): pl.pallas_call(kernel, out_shape=outs, in_specs=[pl.BlockSpec(memory_spac...  9.31 us
  transfers between devices with their start and end apart: 14, of which 6 were waited for; matrix products, arithmetic and copies ran while one was open for 3% of the time, Pallas kernels for 11%

profile of v1, /device:TPU:0, one launch (start us, length us, event | category | flops | bytes accessed | tf_op | source)
XLA Modules:
  0.0 75.1 jit_solution(14752949063754848286)
XLA Ops:
  0.6 3.1 %collective-permute-start.1 = (bf16[256,1024]{1,0:T(8,128)(2,1)}, bf16[256,1024]{1,0:T(8,128)(2,1)S(1)}, u32[]{:S(2)}, u32[]{:S(2)}) collective-permute-start(bf16[256,1024]{1,0:T(8,128)(2,1)} %own.1), channel_id=1, source_target_pairs={{0,1},{1,0},{2,3},{3,2},{4,5},{5,4},{6,7},{7,6},{8,9},{9,8},{10,11... | collective-permute-start | bytes 1572872 | tf_op jit(solution)/shard_map/ppermute | solution.py:20
  4.4 1.0 %dynamic-slice_bitcast_fusion = f32[256,256]{1,0:T(8,128)S(1)} fusion(f32[1,256,1024]{2,1,0:T(8,128)} %param.9, s32[]{:T(128)S(6)} %select_n.10), kind=kLoop, calls=%fused_computation.2 | loop fusion | bytes 524292 | tf_op jit(solution)/shard_map/dynamic_slice | solution.py:250
  5.4 1.1 %fusion = (f32[256,256]{1,0:T(8,128)S(1)}, f32[256,256]{1,0:T(8,128)S(1)}) fusion(f32[256,1024]{1,0:T(8,128)} %bitcast.10), kind=kLoop, calls=%fused_computation.4 | loop fusion | bytes 1048576 | tf_op jit(solution)/shard_map/slice | solution.py:251
  6.6 6.5 %collective-permute-start.4 = (f32[256,768]{1,0:T(8,128)S(1)}, f32[256,768]{1,0:T(8,128)S(1)}, u32[]{:S(2)}, u32[]{:S(2)}) collective-permute-start(f32[256,768]{1,0:T(8,128)S(1)} %pad_maximum_fusion.1), channel_id=1, source_target_pairs={{0,1},{3,2},{4,5},{7,6},{8,9},{11,10},{12,13},{15,14},{16,17},{19,... | collective-permute-start | bytes 2359304 | tf_op jit(solution)/shard_map/ppermute | solution.py:20
  13.2 1.5 %collective-permute-start = (f32[256,768]{1,0:T(8,128)S(1)}, f32[256,768]{1,0:T(8,128)S(1)}, u32[]{:S(2)}, u32[]{:S(2)}) collective-permute-start(f32[256,768]{1,0:T(8,128)S(1)} %pad_maximum_fusion), channel_id=1, source_target_pairs={{0,1},{3,2},{4,5},{7,6},{8,9},{11,10},{12,13},{15,14},{16,17},{19,... | collective-permute-start | bytes 2359304 | tf_op jit(solution)/shard_map/ppermute | solution.py:20
  14.7 1.7 %collective-permute-done.1.end_block.refs_0_.partner = bf16[256,1024]{1,0:T(8,128)(2,1)S(1)} collective-permute-done((bf16[256,1024]{1,0:T(8,128)(2,1)}, bf16[256,1024]{1,0:T(8,128)(2,1)S(1)}, u32[]{:S(2)}, u32[]{:S(2)}) %collective-permute-start.1) | collective-permute-done | bytes 524320 | tf_op jit(solution)/shard_map/ppermute | solution.py:20
  17.1 1.0 %shard_map.77.middle_near = bf16[768,256]{1,0:T(8,128)(2,1)S(1)} custom-call(bf16[256,1024]{1,0:T(8,128)(2,1)S(1)} %collective-permute-done.1.end_block.refs_0_.partner, bf16[256,1024]{1,0:T(8,128)(2,1)S(1)} %copy-done.1, bf16[256,1024]{1,0:T(8,128)(2,1)S(1)} %collective-permute-done.2.other_block.refs_2_.across, f32[256,1024]{1,0:T(8,128)S(1)} %bitcast.11), custom_call_target="tpu_custom_call" | custom-call | flops 1000000000 | bytes 3014656 | tf_op jit(solution)/shard_map/pallas_call | solution.py:86
  18.1 0.7 collective-permute-start.5
  18.8 14.3 %collective-permute-done.4.received = f32[256,768]{1,0:T(8,128)S(1)} collective-permute-done((f32[256,768]{1,0:T(8,128)S(1)}, f32[256,768]{1,0:T(8,128)S(1)}, u32[]{:S(2)}, u32[]{:S(2)}) %collective-permute-start.4) | collective-permute-done | bytes 786464 | tf_op jit(solution)/shard_map/ppermute | solution.py:20
  33.1 1.4 %shard_map.76.of_end = bf16[1024,256]{1,0:T(8,128)(2,1)S(1)} custom-call(bf16[256,1024]{1,0:T(8,128)(2,1)S(1)} %collective-permute-done.1.end_block.refs_0_.partner, bf16[256,1024]{1,0:T(8,128)(2,1)S(1)} %copy-done.1, bf16[256,1024]{1,0:T(8,128)(2,1)S(1)} %collective-permute-done.2.other_block.refs_2_.across, ...), custom_call_target="tpu_custom_call" | custom-call | flops 1000000000 | bytes 4456448 | tf_op jit(solution)/shard_map/pallas_call | solution.py:86
  34.5 0.7 collective-permute-start.7
  35.2 1.3 %collective-permute-start.12 = (bf16[256,1024]{1,0:T(8,128)(2,1)S(1)}, bf16[256,1024]{1,0:T(8,128)(2,1)S(1)}, u32[]{:S(2)}, u32[]{:S(2)}) collective-permute-start(bf16[256,1024]{1,0:T(8,128)(2,1)S(1)} %collective-permute-done.2.other_block.refs_2_.across), channel_id=1, source_target_pairs={{1,0},{2,3},{5,4},{6,7},{9,8},{10,11},{13,12},{14,15},{17,16},{18,... | collective-permute-start | bytes 1572872 | tf_op jit(solution)/shard_map/ppermute | solution.py:20
  36.5 1.3 %collective-permute-start.13 = (bf16[256,1024]{1,0:T(8,128)(2,1)S(1)}, bf16[256,1024]{1,0:T(8,128)(2,1)S(1)}, u32[]{:S(2)}, u32[]{:S(2)}) collective-permute-start(bf16[256,1024]{1,0:T(8,128)(2,1)S(1)} %collective-permute-done.3.last_block.refs_0_.far), channel_id=1, source_target_pairs={{1,0},{2,3},{5,4},{6,7},{9,8},{10,11},{13,12},{14,15},{17,16},{18,... | collective-permute-start | bytes 1572872 | tf_op jit(solution)/shard_map/ppermute | solution.py:20
  38.3 10.6 %collective-permute-done.received = f32[256,768]{1,0:T(8,128)S(1)} collective-permute-done((f32[256,768]{1,0:T(8,128)S(1)}, f32[256,768]{1,0:T(8,128)S(1)}, u32[]{:S(2)}, u32[]{:S(2)}) %collective-permute-start) | collective-permute-done | bytes 786464 | tf_op jit(solution)/shard_map/ppermute | solution.py:20
  49.5 2.0 %shard_map.79 = (f32[256,768]{1,0:T(8,128)S(1)}, bf16[256,768]{1,0:T(8,128)(2,1)S(1)}, f32[8,128]{1,0:T(8,128)S(1)}) custom-call(f32[256,1024]{1,0:T(8,128)S(1)} %bitcast.17, f32[256,768]{1,0:T(8,128)S(1)} %collective-permute-done.received, bf16[1024,256]{1,0:T(8,128)(2,1)S(1)} %shard_map.76.of_end, bf16[768,256]{1,0:T(8,128)(2,1)S(1)} %shard_map.77.middle_near, ...), custom_call_target="tpu_custom_call" | custom-call | flops 1000000000 | bytes 4591616 | tf_op jit(solution)/shard_map/pallas_call | solution.py:86
  51.6 1.3 %collective-permute-start.8 = (bf16[256,768]{1,0:T(8,128)(2,1)S(1)}, bf16[256,768]{1,0:T(8,128)(2,1)S(1)}, u32[]{:S(2)}, u32[]{:S(2)}) collective-permute-start(bf16[256,768]{1,0:T(8,128)(2,1)S(1)} %get-tuple-element.15), channel_id=1, source_target_pairs={{1,0},{2,3},{5,4},{6,7},{9,8},{10,11},{13,12},{14,15},{17,16},{18,... | collective-permute-start | bytes 1179656 | tf_op jit(solution)/shard_map/ppermute | solution.py:20
  52.9 0.9 %shard_map.80 = (f32[256,256]{1,0:T(8,128)S(1)}, bf16[272,256]{1,0:T(8,128)(2,1)S(1)}, f32[8,128]{1,0:T(8,128)S(1)}) custom-call(f32[256,1024]{1,0:T(8,128)S(1)} %bitcast.18, f32[256,768]{1,0:T(8,128)S(1)} %collective-permute-done.received, bf16[1024,256]{1,0:T(8,128)(2,1)S(1)} %collective-permute-done.7.of_last, f32[8,128]{1,0:T(8,128)S(1)} %get-tuple-element.13.before), custom_call_target="tpu_custom_call" | custom-call | flops 1000000000 | bytes 2768896 | tf_op jit(solution)/shard_map/pallas_call | solution.py:86
  53.8 1.3 %collective-permute-start.9 = (bf16[272,256]{1,0:T(8,128)(2,1)S(1)}, bf16[272,256]{1,0:T(8,128)(2,1)S(1)}, u32[]{:S(2)}, u32[]{:S(2)}) collective-permute-start(bf16[272,256]{1,0:T(8,128)(2,1)S(1)} %get-tuple-element.16), channel_id=1, source_target_pairs={{1,0},{2,3},{5,4},{6,7},{9,8},{10,11},{13,12},{14,15},{17,16},{18,... | collective-permute-start | bytes 417800 | tf_op jit(solution)/shard_map/ppermute | solution.py:20
  55.8 1.3 %collective-permute-start.11 = (f32[8,128]{1,0:T(8,128)S(1)}, f32[8,128]{1,0:T(8,128)S(1)}, u32[]{:S(2)}, u32[]{:S(2)}) collective-permute-start(f32[8,128]{1,0:T(8,128)S(1)} %get-tuple-element.17.square), channel_id=1, source_target_pairs={{2,0},{1,3},{6,4},{5,7},{10,8},{9,11},{14,12},{13,15},{18,16},{17,... | collective-permute-start | bytes 12296 | tf_op jit(solution)/shard_map/ppermute | solution.py:20
  57.1 8.0 %collective-permute-done.13.in_far = bf16[256,1024]{1,0:T(8,128)(2,1)S(1)} collective-permute-done((bf16[256,1024]{1,0:T(8,128)(2,1)S(1)}, bf16[256,1024]{1,0:T(8,128)(2,1)S(1)}, u32[]{:S(2)}, u32[]{:S(2)}) %collective-permute-start.13) | collective-permute-done | bytes 524320 | tf_op jit(solution)/shard_map/ppermute | solution.py:20
  65.1 2.5 %shard_map.81 = (f32[256,1024]{1,0:T(8,128)}, f32[256,1024]{1,0:T(8,128)}, f32[8,128]{1,0:T(8,128)S(1)}) custom-call(bf16[256,1024]{1,0:T(8,128)(2,1)S(1)} %copy-done.1, bf16[256,1024]{1,0:T(8,128)(2,1)S(1)} %collective-permute-done.1.end_block.refs_0_.partner, bf16[256,1024]{1,0:T(8,128)(2,1)S(1)} %collective-permute-done.2.other_block.refs_2_.across, ...), custom_call_target="tpu_custom_call" | custom-call | flops 1000000000 | bytes 7344128 | tf_op jit(solution)/shard_map/pallas_call | solution.py:86
  67.6 5.0 %collective-permute-done.8.back = bf16[256,768]{1,0:T(8,128)(2,1)S(1)} collective-permute-done((bf16[256,768]{1,0:T(8,128)(2,1)S(1)}, bf16[256,768]{1,0:T(8,128)(2,1)S(1)}, u32[]{:S(2)}, u32[]{:S(2)}) %collective-permute-start.8) | collective-permute-done | bytes 393248 | tf_op jit(solution)/shard_map/ppermute | solution.py:20
  72.7 1.5 %collective-permute-done.9.back_last = bf16[272,256]{1,0:T(8,128)(2,1)S(1)} collective-permute-done((bf16[272,256]{1,0:T(8,128)(2,1)S(1)}, bf16[272,256]{1,0:T(8,128)(2,1)S(1)}, u32[]{:S(2)}, u32[]{:S(2)}) %collective-permute-start.9) | collective-permute-done | bytes 139296 | tf_op jit(solution)/shard_map/ppermute | solution.py:20
  74.1 1.0 %shard_map.82 = bf16[256,1024]{1,0:T(8,128)(2,1)} custom-call(f32[256,768]{1,0:T(8,128)S(1)} %get-tuple-element.12.kept, f32[256,256]{1,0:T(8,128)S(1)} %get-tuple-element.14.kept_last, bf16[256,768]{1,0:T(8,128)(2,1)S(1)} %collective-permute-done.8.back, bf16[272,256]{1,0:T(8,128)(2,1)S(1)} %collective-permute-done.9.back_last, ...), custom_call_target="tpu_custom_call" | custom-call | flops 1000000 | bytes 2121728 | tf_op jit(solution)/shard_map/pallas_call | solution.py:86
  (27 shorter events, 3.4 us)
Async XLA Ops:
  0.6 15.7 %collective-permute-start.1 = (bf16[256,1024]{1,0:T(8,128)(2,1)}, bf16[256,1024]{1,0:T(8,128)(2,1)S(1)}, u32[]{:S(2)}, u32[]{:S(2)}) collective-permute-start(bf16[256,1024]{1,0:T(8,128)(2,1)} %own.1), channel_id=1, source_target_pairs={{0,1},{1,0},{2,3},{3,2},{4,5},{5,4},{6,7},{7,6},{8,9},{9,8},{10,11... | collective-permute-start | bytes 1572872 | tf_op jit(solution)/shard_map/ppermute | solution.py:20
  3.7 13.3 %collective-permute-start.2 = (bf16[256,1024]{1,0:T(8,128)(2,1)}, bf16[256,1024]{1,0:T(8,128)(2,1)S(1)}, u32[]{:S(2)}, u32[]{:S(2)}) collective-permute-start(bf16[256,1024]{1,0:T(8,128)(2,1)} %own.1), channel_id=1, source_target_pairs={{1,2},{2,1},{5,6},{6,5},{9,10},{10,9},{13,14},{14,13},{17,18},{18,... | collective-permute-start | bytes 1572872 | tf_op jit(solution)/shard_map/ppermute | solution.py:20
  6.5 6.5 %copy-start.4 = (f32[1,256,1024]{2,1,0:T(8,128)S(1)}, f32[1,256,1024]{2,1,0:T(8,128)}, u32[]{:S(2)}) copy-start(f32[1,256,1024]{2,1,0:T(8,128)} %param.8) | copy-start | bytes 3145732
  6.6 26.6 %collective-permute-start.4 = (f32[256,768]{1,0:T(8,128)S(1)}, f32[256,768]{1,0:T(8,128)S(1)}, u32[]{:S(2)}, u32[]{:S(2)}) collective-permute-start(f32[256,768]{1,0:T(8,128)S(1)} %pad_maximum_fusion.1), channel_id=1, source_target_pairs={{0,1},{3,2},{4,5},{7,6},{8,9},{11,10},{12,13},{15,14},{16,17},{19,... | collective-permute-start | bytes 2359304 | tf_op jit(solution)/shard_map/ppermute | solution.py:20
  13.1 4.0 %copy-start = (f32[1,256,1024]{2,1,0:T(8,128)S(1)}, f32[1,256,1024]{2,1,0:T(8,128)}, u32[]{:S(2)}) copy-start(f32[1,256,1024]{2,1,0:T(8,128)} %param.9) | copy-start | bytes 3145732
  13.1 4.0 %copy-start.1 = (bf16[256,1024]{1,0:T(8,128)(2,1)S(1)}, bf16[256,1024]{1,0:T(8,128)(2,1)}, u32[]{:S(2)}) copy-start(bf16[256,1024]{1,0:T(8,128)(2,1)} %own.1) | copy-start | bytes 1572868
  13.2 35.6 %collective-permute-start = (f32[256,768]{1,0:T(8,128)S(1)}, f32[256,768]{1,0:T(8,128)S(1)}, u32[]{:S(2)}, u32[]{:S(2)}) collective-permute-start(f32[256,768]{1,0:T(8,128)S(1)} %pad_maximum_fusion), channel_id=1, source_target_pairs={{0,1},{3,2},{4,5},{7,6},{8,9},{11,10},{12,13},{15,14},{16,17},{19,... | collective-permute-start | bytes 2359304 | tf_op jit(solution)/shard_map/ppermute | solution.py:20
  16.4 16.8 %collective-permute-start.3 = (bf16[256,1024]{1,0:T(8,128)(2,1)S(1)}, bf16[256,1024]{1,0:T(8,128)(2,1)S(1)}, u32[]{:S(2)}, u32[]{:S(2)}) collective-permute-start(bf16[256,1024]{1,0:T(8,128)(2,1)S(1)} %collective-permute-done.1.end_block.refs_0_.partner), channel_id=1, source_target_pairs={{1,2},{2,1},{5,6},{6,5},{9,10},{10,9},{13,14},{14,13},{17,18},{18,... | collective-permute-start | bytes 1572872 | tf_op jit(solution)/shard_map/ppermute | solution.py:20
  18.1 31.4 %collective-permute-start.5 = (bf16[768,256]{1,0:T(8,128)(2,1)S(1)}, bf16[768,256]{1,0:T(8,128)(2,1)S(1)}, u32[]{:S(2)}, u32[]{:S(2)}) collective-permute-start(bf16[768,256]{1,0:T(8,128)(2,1)S(1)} %shard_map.77.middle_near), channel_id=1, source_target_pairs={{1,2},{2,1},{5,6},{6,5},{9,10},{10,9},{13,14},{14,13},{17,18},{18,... | collective-permute-start | bytes 1179656 | tf_op jit(solution)/shard_map/ppermute | solution.py:20
  34.5 18.4 %collective-permute-start.7 = (bf16[1024,256]{1,0:T(8,128)(2,1)S(1)}, bf16[1024,256]{1,0:T(8,128)(2,1)S(1)}, u32[]{:S(2)}, u32[]{:S(2)}) collective-permute-start(bf16[1024,256]{1,0:T(8,128)(2,1)S(1)} %shard_map.76.of_end), channel_id=1, source_target_pairs={{1,2},{2,1},{5,6},{6,5},{9,10},{10,9},{13,14},{14,13},{17,18},{18,... | collective-permute-start | bytes 1572872 | tf_op jit(solution)/shard_map/ppermute | solution.py:20
  35.2 20.6 %collective-permute-start.12 = (bf16[256,1024]{1,0:T(8,128)(2,1)S(1)}, bf16[256,1024]{1,0:T(8,128)(2,1)S(1)}, u32[]{:S(2)}, u32[]{:S(2)}) collective-permute-start(bf16[256,1024]{1,0:T(8,128)(2,1)S(1)} %collective-permute-done.2.other_block.refs_2_.across), channel_id=1, source_target_pairs={{1,0},{2,3},{5,4},{6,7},{9,8},{10,11},{13,12},{14,15},{17,16},{18,... | collective-permute-start | bytes 1572872 | tf_op jit(solution)/shard_map/ppermute | solution.py:20
  36.5 28.6 %collective-permute-start.13 = (bf16[256,1024]{1,0:T(8,128)(2,1)S(1)}, bf16[256,1024]{1,0:T(8,128)(2,1)S(1)}, u32[]{:S(2)}, u32[]{:S(2)}) collective-permute-start(bf16[256,1024]{1,0:T(8,128)(2,1)S(1)} %collective-permute-done.3.last_block.refs_0_.far), channel_id=1, source_target_pairs={{1,0},{2,3},{5,4},{6,7},{9,8},{10,11},{13,12},{14,15},{17,16},{18,... | collective-permute-start | bytes 1572872 | tf_op jit(solution)/shard_map/ppermute | solution.py:20
  48.8 0.7 collective-permute-start.6
  51.6 21.1 %collective-permute-start.8 = (bf16[256,768]{1,0:T(8,128)(2,1)S(1)}, bf16[256,768]{1,0:T(8,128)(2,1)S(1)}, u32[]{:S(2)}, u32[]{:S(2)}) collective-permute-start(bf16[256,768]{1,0:T(8,128)(2,1)S(1)} %get-tuple-element.15), channel_id=1, source_target_pairs={{1,0},{2,3},{5,4},{6,7},{9,8},{10,11},{13,12},{14,15},{17,16},{18,... | collective-permute-start | bytes 1179656 | tf_op jit(solution)/shard_map/ppermute | solution.py:20
  52.9 12.2 %copy-start.2 = (f32[1,256,1024]{2,1,0:T(8,128)S(1)}, f32[1,256,1024]{2,1,0:T(8,128)}, u32[]{:S(2)}) copy-start(f32[1,256,1024]{2,1,0:T(8,128)} %param.6) | copy-start | bytes 3145732
  52.9 12.2 %copy-start.3 = (f32[1,256,1024]{2,1,0:T(8,128)S(1)}, f32[1,256,1024]{2,1,0:T(8,128)}, u32[]{:S(2)}) copy-start(f32[1,256,1024]{2,1,0:T(8,128)} %param.7) | copy-start | bytes 3145732
  53.8 20.3 %collective-permute-start.9 = (bf16[272,256]{1,0:T(8,128)(2,1)S(1)}, bf16[272,256]{1,0:T(8,128)(2,1)S(1)}, u32[]{:S(2)}, u32[]{:S(2)}) collective-permute-start(bf16[272,256]{1,0:T(8,128)(2,1)S(1)} %get-tuple-element.16), channel_id=1, source_target_pairs={{1,0},{2,3},{5,4},{6,7},{9,8},{10,11},{13,12},{14,15},{17,16},{18,... | collective-permute-start | bytes 417800 | tf_op jit(solution)/shard_map/ppermute | solution.py:20
  55.1 17.5 %collective-permute-start.10 = (f32[8,128]{1,0:T(8,128)S(1)}, f32[8,128]{1,0:T(8,128)S(1)}, u32[]{:S(2)}, u32[]{:S(2)}) collective-permute-start(f32[8,128]{1,0:T(8,128)S(1)} %get-tuple-element.17.square), channel_id=1, source_target_pairs={{1,2},{2,1},{5,6},{6,5},{9,10},{10,9},{13,14},{14,13},{17,18},{18,... | collective-permute-start | bytes 12296 | tf_op jit(solution)/shard_map/ppermute | solution.py:20
  55.8 16.8 %collective-permute-start.11 = (f32[8,128]{1,0:T(8,128)S(1)}, f32[8,128]{1,0:T(8,128)S(1)}, u32[]{:S(2)}, u32[]{:S(2)}) collective-permute-start(f32[8,128]{1,0:T(8,128)S(1)} %get-tuple-element.17.square), channel_id=1, source_target_pairs={{2,0},{1,3},{6,4},{5,7},{10,8},{9,11},{14,12},{13,15},{18,16},{17,... | collective-permute-start | bytes 12296 | tf_op jit(solution)/shard_map/ppermute | solution.py:20
